TPU v7x, 32 devices: a whole 2x2x4 slice. The times are simulated.
32 devices in a mesh: dp: 8 (over z, x), rep: 4 (over y, core).
Axes of the slice: x: 2, y: 2, z: 4, core: 2. Of those that a mesh axis runs over, the one named last changes fastest.
Arguments:
- features: bfloat16 [5120, 8192], P('dp', 'rep'), may hold values from -6 to 6
- out_grads: bfloat16 [5120, 1024], P('dp'), may hold values from -12 to 12, as said below
- cold_sums: bfloat16 [8, 8192, 1024], P('dp', 'rep'), may hold values from -96 to 96
- weight: float32 [8192, 1024], P(('rep', 'dp')), may hold values from -3 to 3
- moment: float32 [8192, 1024], P(('rep', 'dp')), may hold values from -6 to 6
- second: float32 [8192, 1024], P(('rep', 'dp')), may hold values from 0.01 to 4
- ranks: int32 [8], replicated, may hold values from 0 to 7, each once
Outputs:
- new_weight: float32 [8192, 1024], P(('rep', 'dp'))
- new_moment: float32 [8192, 1024], P(('rep', 'dp'))
- new_second: float32 [8192, 1024], P(('rep', 'dp'))
- new_cold: bfloat16 [8, 8192, 1024], P('dp', 'rep')
- column_sq: float32 [1024], replicated
Inputs may be any that keep to these rules, and one draw needn't show every extreme that they name: `ranks`: each block number appears once. `out_grads`: column scales differ from column to column.
All inputs are finite; a program needn't handle non-finite values.
Results may differ from a plain program's by a relative error of at most 0.001.
Values sent between devices are 32-bit elements; how exact they have to be, the bound alone decides.
No kernel may reach another device: no remote copies, remote signals or barrier semaphores. Data moves between devices by JAX's collectives and lax.ppermute only.
A program may use at most 128 MiB of HBM per device.

v0:
```python
import jax
import jax.numpy as jnp
from jax import lax
from jax.sharding import PartitionSpec as P


def body(features, out_grads, cold_sums, weight, moment, second, ranks):
    blocks = ranks.shape[0]
    hot_count = blocks // 2
    width = out_grads.shape[1]
    local_rows = features.shape[1]
    grad = lax.dot_general(
        features, out_grads, (((0,), (0,)), ((), ())), preferred_element_type=jnp.float32
    )
    local = cold_sums[0].astype(jnp.float32) + grad
    hot_block = ranks < hot_count
    hot_col = jnp.repeat(hot_block, 128)
    new_cold = jnp.where(hot_col[None, :], jnp.float32(0.0), local).astype(jnp.bfloat16)[None]
    partial_sq = jnp.sum(local * local, axis=0)
    column_sq = lax.psum(partial_sq, ("dp", "rep"))
    picker = (ranks[None, :] == jnp.arange(hot_count, dtype=jnp.int32)[:, None]).astype(jnp.float32)
    packed = jnp.einsum(
        "rbk,sb->rsk",
        local.reshape(local_rows, blocks, 128),
        picker,
        precision=lax.Precision.HIGHEST,
    )
    owned = lax.psum_scatter(
        packed.reshape(local_rows, hot_count * 128), "dp", scatter_dimension=0, tiled=True
    )
    owned_rows = owned.shape[0]
    spread = jnp.einsum(
        "rsk,sb->rbk",
        owned.reshape(owned_rows, hot_count, 128),
        picker,
        precision=lax.Precision.HIGHEST,
    )
    summed = spread.reshape(owned_rows, width)
    dp_count = lax.axis_size("dp")
    total_rows = local_rows * lax.axis_size("rep")
    rms = jnp.sqrt(column_sq / jnp.float32(total_rows * dp_count * features.shape[0]))
    clip = 1.0 / jnp.maximum(jnp.float32(1.0), rms)
    grad_mean = summed * clip[None, :] / jnp.float32(dp_count)
    moved = 0.9 * moment + 0.1 * grad_mean
    squared = 0.95 * second + 0.05 * grad_mean * grad_mean
    step_size = 0.05 * (moved / (1.0 - 0.9**10)) / (jnp.sqrt(squared / (1.0 - 0.95**10)) + 1e-08)
    new_moment = jnp.where(hot_col[None, :], moved, moment)
    new_second = jnp.where(hot_col[None, :], squared, second)
    new_weight = jnp.where(hot_col[None, :], weight - step_size, weight)
    return (new_weight, new_moment, new_second, new_cold, column_sq)


def solution(mesh):
    placed = (
        P("dp", "rep"),
        P("dp", None),
        P("dp", "rep", None),
        P(("rep", "dp"), None),
        P(("rep", "dp"), None),
        P(("rep", "dp"), None),
        P(),
    )
    return jax.shard_map(
        body,
        mesh=mesh,
        in_specs=placed,
        out_specs=(
            P(("rep", "dp"), None),
            P(("rep", "dp"), None),
            P(("rep", "dp"), None),
            P("dp", "rep", None),
            P(),
        ),
        check_vma=False,
    )
```

profile of v0, /device:TPU:0, one launch (start us, length us, event | category | flops | bytes accessed | tf_op | source)
XLA Modules:
  0.0 146.8 jit_solution(3876229552257421479)
XLA Ops:
  7.2 0.0 copy-start
  7.2 0.0 reduce-scatter.2.cloned.1.call-start
  7.2 6.6 %copy.12 = bf16[1,2048,1024]{1,2,0:T(8,128)(2,1)} copy(bf16[1,2048,1024]{2,1,0:T(8,128)(2,1)} %param.9) | data formatting | bytes 8388608 | tf_op args[2]
  13.8 0.0 copy-done
  13.8 8.0 %multiply_reduce_fusion = (f32[1024]{0:T(1024)S(1)}, f32[2048,1024]{0,1:T(8,128)}) fusion(bf16[640,2048]{1,0:T(8,128)(2,1)S(1)} %copy-done, bf16[640,1024]{1,0:T(8,128)(2,1)} %param.8, bf16[1,2048,1024]{1,2,0:T(8,128)(2,1)} %copy.12), kind=kOutput, calls=%fused_computation.2 | convolution fusion | flops 2692742144 | bytes 16519168 | tf_op jit(solution)/shard_map/dot_general | solution.py:12
  21.8 0.0 copy-start.2
  21.8 9.3 %copy.13 = f32[2048,8,128]{2,1,0:T(8,128)} copy(f32[2048,8,128]{0,2,1:T(8,128)} %bitcast.37) | data formatting | bytes 16777216 | tf_op jit(solution)/shard_map/reshape | solution.py:24
  31.1 0.0 copy-done.2
  31.1 7.4 %fusion.6 = f32[4,2048,128]{2,0,1:T(4,128)S(1)} fusion(f32[2048,8,128]{2,1,0:T(8,128)} %copy.13, s32[8]{0:T(128)S(1)} %copy-done.2), kind=kOutput, calls=%fused_computation.16 | convolution fusion | flops 100663328 | bytes 12582944 | tf_op jit(solution)/shard_map/rbk,sb->rsk/dot_general | solution.py:22
  38.6 2.4 %copy.31 = f32[256,8,4,128]{3,1,2,0:T(8,128)} copy(f32[256,8,4,128]{3,2,1,0:T(4,128)S(1)} %bitcast.39) | data formatting | bytes 8388608
  41.0 0.0 reduce-scatter.2.cloned.1.call-update
  41.0 0.1 broadcast_bitcast_fusion
  41.1 5.9 %fusion = bf16[1,2048,1024]{1,2,0:T(8,128)(2,1)} fusion(f32[2048,1024]{0,1:T(8,128)} %get-tuple-element.14, pred[1024]{0:T(1024)(128)(4,1)S(1)} %broadcast_bitcast_fusion), kind=kLoop, calls=%fused_computation.3 | loop fusion | flops 2097152 | bytes 12583936 | tf_op jit(solution)/shard_map/broadcast_in_dim | solution.py:18
  47.0 6.4 %copy.14 = bf16[1,2048,1024]{2,1,0:T(8,128)(2,1)} copy(bf16[1,2048,1024]{1,2,0:T(8,128)(2,1)} %fusion) | data formatting | bytes 8388608
  53.4 43.8 %psum.7 = f32[1024]{0:T(1024)S(1)} all-reduce(f32[1024]{0:T(1024)S(1)} %get-tuple-element.13), channel_id=1, replica_groups=mesh['dp'=8,'rep'=4] {'dp','rep'}, use_global_device_ids=true, to_apply=%region_2.3 | all-reduce | flops 1024 | bytes 8192 | tf_op jit(solution)/shard_map/psum | solution.py:20
  97.2 0.0 copy-start.1
  97.2 36.1 %reduce-scatter.2.cloned.1.call-done = f32[256,512]{1,0:T(8,128)} async-done(((f32[2048,512]{1,0:T(8,128)}), f32[256,512]{1,0:T(8,128)}) %reduce-scatter.2.cloned.1.call-update) | async-done | bytes 524304 | tf_op jit(solution)/shard_map/reduce_scatter | solution.py:28
  133.3 1.2 reshape.29
  134.5 0.7 fusion.4
  135.3 4.6 %fusion.2 = (f32[256,1024]{1,0:T(8,128)}, f32[256,1024]{1,0:T(8,128)}, f32[256,1024]{1,0:T(8,128)}) fusion(f32[256,1024]{1,0:T(8,128)} %param.12, f32[32,8,8,128]{3,2,1,0:T(8,128)S(1)} %bitcast.40, f32[1024]{0:T(1024)S(1)} %maximum_divide_fusion, pred[1024]{0:T(1024)(128)(4,1)S(1)} %broadcast_bitcast_fusion, f32[256,1024]{1,0:T(8,128)} %param.10, ...), kind=kLoop, calls=%fused_computation.10 | loop fusion | flops 4456448 | bytes 7345152 | tf_op jit(solution)/shard_map/jit(_where)/select_n | solution.py:48
  139.9 0.0 copy-done.1
  (2 shorter events, 0.0 us)
Async XLA Ops:
  7.2 6.6 %copy-start = (bf16[640,2048]{1,0:T(8,128)(2,1)S(1)}, bf16[640,2048]{1,0:T(8,128)(2,1)}, u32[]{:S(2)}) copy-start(bf16[640,2048]{1,0:T(8,128)(2,1)} %param.7) | copy-start | bytes 7864324
  7.2 126.1 %reduce-scatter.2.cloned.1.call-start = ((), (), s32[]{:S(2)}) async-start(), calls=%async_computation.1 | async-start | bytes 4718592 | tf_op jit(solution)/shard_map/reduce_scatter | solution.py:28
  21.8 9.3 %copy-start.2 = (s32[8]{0:T(128)S(1)}, s32[8]{0:T(128)}, u32[]{:S(2)}) copy-start(s32[8]{0:T(128)} %param.13) | copy-start | bytes 100
  97.2 42.7 %copy-start.1 = (f32[1024]{0:T(1024)}, f32[1024]{0:T(1024)S(1)}, u32[]{:S(2)}) copy-start(f32[1024]{0:T(1024)S(1)} %psum.7) | copy-start | bytes 12292
Sparse Core Ops, SparseCore 0:
  41.1 92.1 reduce-scatter.1
where the time goes:
time: 147 us
  blocking collectives  43.8 us (30%)
  waiting for transfers between devices  36.1 us (25%)
  local copies, waits for them, and re-layouts  26 us (18%)
  matrix products  16.2 us (11%)
  between operations  14.1 us (10%)
  other arithmetic  10.5 us (7%)
    psum x1, blocking collectives, body(): column_sq = lax.psum(partial_sq, ('dp', 'rep'))  43.8 us
    reduce_scatter x1, waiting for transfers between devices, body(): lax.psum_scatter(packed.reshape(local_rows, hot_count * 128), 'dp', scatt...  36.1 us
    unnamed x9, local copies, waits for them, and re-layouts  15.4 us
    reshape x1, local copies, waits for them, and re-layouts, body(): local.reshape(local_rows, blocks, 128)  9.3 us
    dot_general x1, matrix products, body(): lax.dot_general(features, out_grads, (((0,), (0,)), ((), ())), preferred_...  8.02 us
    dot_general x1, matrix products, body(): jnp.einsum('rbk,sb->rsk', local.reshape(local_rows, blocks, 128), picker,...  7.42 us
    broadcast_in_dim x1, other arithmetic, body(): jnp.where(hot_col[None, :], jnp.float32(0.0), local).astype(jnp.bfloat16)  5.88 us
    select_n x1, other arithmetic, body(): new_second = jnp.where(hot_col[None, :], squared, second)  4.64 us
  transfers between devices with their start and end apart: 1, of which 1 were waited for; matrix products, arithmetic and copies ran while one was open for 8% of the time, Pallas kernels for 0%

commit v1 on v0

--- a/solution.py
+++ b/solution.py
@@ -2,6 +2,10 @@
 import jax.numpy as jnp
 from jax import lax
 from jax.sharding import PartitionSpec as P
+
+
+def cycle(count):
+    return list(range(1, count, 2)) + list(reversed(range(0, count, 2)))
 
 
 def body(features, out_grads, cold_sums, weight, moment, second, ranks):
@@ -25,8 +29,11 @@
         picker,
         precision=lax.Precision.HIGHEST,
     )
+    members = cycle(lax.axis_size("dp"))
+    part = packed.reshape(len(members), local_rows // len(members), hot_count * 128)
+    ordered = jnp.concatenate([part[m] for m in members], axis=0)
     owned = lax.psum_scatter(
-        packed.reshape(local_rows, hot_count * 128), "dp", scatter_dimension=0, tiled=True
+        ordered, "dp", scatter_dimension=0, tiled=True, axis_index_groups=[members]
     )
     owned_rows = owned.shape[0]
     spread = jnp.einsum(

time: 147 us -> 116 us (0.79)
  waiting for transfers between devices: 36.1 us -> 0.04 us
  local copies, waits for them, and re-layouts: 26 us -> 30.5 us
    reduce_scatter x1, waiting for transfers between devices: 36.1 us -> 0.02 us  [body(): lax.psum_scatter(ordered, 'dp', scatter_dimension=0, tiled=True, axis_ind...]
    unnamed x9 -> x15, local copies, waits for them, and re-layouts: 15.4 us -> 18.8 us
  transfers between devices with their start and end apart: 1 -> 1, of which waited for: 1 -> 0; matrix products, arithmetic and copies ran while one was open for 8% -> 11% of each run, Pallas kernels for 0% -> 0%
where the time goes in v1:
time: 116 us
  blocking collectives  44.1 us (38%)
  local copies, waits for them, and re-layouts  30.5 us (26%)
  matrix products  16.3 us (14%)
  between operations  14.1 us (12%)
  other arithmetic  10.5 us (9%)
    psum x1, blocking collectives, body(): column_sq = lax.psum(partial_sq, ('dp', 'rep'))  44.1 us
    unnamed x15, local copies, waits for them, and re-layouts  18.8 us
    reshape x1, local copies, waits for them, and re-layouts, body(): local.reshape(local_rows, blocks, 128)  9.29 us
    dot_general x1, matrix products, body(): lax.dot_general(features, out_grads, (((0,), (0,)), ((), ())), preferred_...  8.15 us
    dot_general x1, matrix products, body(): jnp.einsum('rbk,sb->rsk', local.reshape(local_rows, blocks, 128), picker,...  7.42 us
    broadcast_in_dim x1, other arithmetic, body(): jnp.where(hot_col[None, :], jnp.float32(0.0), local).astype(jnp.bfloat16)  5.87 us
    select_n x1, other arithmetic, body(): new_second = jnp.where(hot_col[None, :], squared, second)  4.64 us
  transfers between devices with their start and end apart: 1, of which 0 were waited for; matrix products, arithmetic and copies ran while one was open for 11% of the time, Pallas kernels for 0%

profile of v1, /device:TPU:0, one launch (start us, length us, event | category | flops | bytes accessed | tf_op | source)
XLA Modules:
  0.0 115.6 jit_solution(7516741653848244742)
XLA Ops:
  7.2 0.0 copy-start
  7.2 0.0 reduce-scatter.2.cloned.1.call-start
  7.2 6.6 %copy.12 = bf16[1,2048,1024]{1,2,0:T(8,128)(2,1)} copy(bf16[1,2048,1024]{2,1,0:T(8,128)(2,1)} %param.9) | data formatting | bytes 8388608 | tf_op args[2]
  13.8 0.0 copy-done
  13.8 8.2 %multiply_reduce_fusion = (f32[1024]{0:T(1024)S(1)}, f32[2048,1024]{0,1:T(8,128)}) fusion(bf16[640,2048]{1,0:T(8,128)(2,1)S(1)} %copy-done, bf16[640,1024]{1,0:T(8,128)(2,1)} %param.8, bf16[1,2048,1024]{1,2,0:T(8,128)(2,1)} %copy.12), kind=kOutput, calls=%fused_computation.2 | convolution fusion | flops 2692742144 | bytes 16519168 | tf_op jit(solution)/shard_map/dot_general | solution.py:16
  22.0 0.0 copy-start.2
  22.0 9.3 %copy.13 = f32[2048,8,128]{2,1,0:T(8,128)} copy(f32[2048,8,128]{0,2,1:T(8,128)} %bitcast.58) | data formatting | bytes 16777216 | tf_op jit(solution)/shard_map/reshape | solution.py:28
  31.3 0.0 copy-done.2
  31.3 7.4 %convolution_bitcast_fusion = f32[2048,4,128]{2,1,0:T(4,128)S(1)} fusion(f32[2048,8,128]{2,1,0:T(8,128)} %copy.13, s32[8]{0:T(128)S(1)} %copy-done.2), kind=kOutput, calls=%fused_computation.4 | convolution fusion | flops 100663328 | bytes 12582944 | tf_op jit(solution)/shard_map/rbk,sb->rsk/dot_general | solution.py:26
  38.7 0.3 fusion.9
  39.0 0.9 bitcast_dynamic-update-slice_fusion.7
  39.8 0.9 bitcast_dynamic-update-slice_fusion.6
  40.7 0.8 bitcast_dynamic-update-slice_fusion.5
  41.6 0.8 bitcast_dynamic-update-slice_fusion.4
  42.4 0.9 bitcast_dynamic-update-slice_fusion.3
  43.3 0.8 bitcast_dynamic-update-slice_fusion.2
  44.1 0.8 bitcast_dynamic-update-slice_fusion.1
  44.9 0.8 bitcast_dynamic-update-slice_fusion
  45.8 0.0 reduce-scatter.2.cloned.1.call-update
  45.8 0.1 broadcast_bitcast_fusion
  45.9 5.9 %fusion = bf16[1,2048,1024]{1,2,0:T(8,128)(2,1)} fusion(f32[2048,1024]{0,1:T(8,128)} %get-tuple-element.22, pred[1024]{0:T(1024)(128)(4,1)S(1)} %broadcast_bitcast_fusion), kind=kLoop, calls=%fused_computation.3 | loop fusion | flops 2097152 | bytes 12583936 | tf_op jit(solution)/shard_map/broadcast_in_dim | solution.py:22
  51.8 6.3 %copy.14 = bf16[1,2048,1024]{2,1,0:T(8,128)(2,1)} copy(bf16[1,2048,1024]{1,2,0:T(8,128)(2,1)} %fusion) | data formatting | bytes 8388608
  58.1 44.1 %psum.7 = f32[1024]{0:T(1024)S(1)} all-reduce(f32[1024]{0:T(1024)S(1)} %get-tuple-element.21), channel_id=1, replica_groups=mesh['dp'=8,'rep'=4] {'dp','rep'}, use_global_device_ids=true, to_apply=%region_2.3 | all-reduce | flops 1024 | bytes 8192 | tf_op jit(solution)/shard_map/psum | solution.py:24
  102.1 0.0 copy-start.1
  102.1 0.0 reduce-scatter.2.cloned.1.call-done
  102.1 1.2 %reshape.42 = f32[256,4,128]{2,1,0:T(4,128)S(1)} reshape(f32[256,512]{1,0:T(8,128)} %reduce-scatter.2.cloned.1.call-done) | data formatting | bytes 1048576 | tf_op jit(solution)/shard_map/reshape | solution.py:41
  103.4 0.7 fusion.4
  104.1 4.6 %fusion.2 = (f32[256,1024]{1,0:T(8,128)}, f32[256,1024]{1,0:T(8,128)}, f32[256,1024]{1,0:T(8,128)}) fusion(f32[256,1024]{1,0:T(8,128)} %param.12, f32[32,8,8,128]{3,2,1,0:T(8,128)S(1)} %bitcast.59, f32[1024]{0:T(1024)S(1)} %maximum_divide_fusion, pred[1024]{0:T(1024)(128)(4,1)S(1)} %broadcast_bitcast_fusion, f32[256,1024]{1,0:T(8,128)} %param.10, ...), kind=kLoop, calls=%fused_computation.10 | loop fusion | flops 4456448 | bytes 7345152 | tf_op jit(solution)/shard_map/jit(_where)/select_n | solution.py:55
  108.7 0.0 copy-done.1
  (2 shorter events, 0.0 us)
Async XLA Ops:
  7.2 6.6 %copy-start = (bf16[640,2048]{1,0:T(8,128)(2,1)S(1)}, bf16[640,2048]{1,0:T(8,128)(2,1)}, u32[]{:S(2)}) copy-start(bf16[640,2048]{1,0:T(8,128)(2,1)} %param.7) | copy-start | bytes 7864324
  7.2 95.0 %reduce-scatter.2.cloned.1.call-start = ((), (), s32[]{:S(2)}) async-start(), calls=%async_computation.1 | async-start | bytes 4718592 | tf_op jit(solution)/shard_map/reduce_scatter | solution.py:35
  22.0 9.3 %copy-start.2 = (s32[8]{0:T(128)S(1)}, s32[8]{0:T(128)}, u32[]{:S(2)}) copy-start(s32[8]{0:T(128)} %param.13) | copy-start | bytes 100
  102.1 6.6 %copy-start.1 = (f32[1024]{0:T(1024)}, f32[1024]{0:T(1024)S(1)}, u32[]{:S(2)}) copy-start(f32[1024]{0:T(1024)S(1)} %psum.7) | copy-start | bytes 12292
Sparse Core Ops, SparseCore 0:
  45.9 52.1 reduce-scatter.1
